TPU v7x, 32 devices: a whole 2x2x4 slice. The times are simulated.
32 devices in a mesh: row: 8 (over y, x, core), col: 4 (over z).
Axes of the slice: x: 2, y: 2, z: 4, core: 2. Of those that a mesh axis runs over, the one named last changes fastest.
Arguments:
- density_start: float32 [512, 512], P('row', 'col'), may hold values from -0.5 to 1, as said below
- branches: int32 [6], replicated, may hold values from 0 to 1, as said below
Outputs:
- density: float32 [512, 512], P('row', 'col')
- occupations: float32 [6, 2], replicated
Inputs may be any that keep to these rules, and one draw needn't show every extreme that they name: density_start is symmetric with eigenvalues inside 0 to 1. `branches`: each entry is 0 or 1, and exactly 3 entries are 1.
All inputs are finite; a program needn't handle non-finite values.
Results may differ from a plain program's by a relative error of at most 0.0025.
Values may be sent and summed in bfloat16 or wider, within the bound.
A program may use at most 64 MiB of HBM per device.

v0:
```python
import jax
import jax.numpy as jnp
from jax import lax
from jax.sharding import PartitionSpec as P

ITERS = 6


def taken_in(shard, axis, dim, absorb, state):
    everything = jax.tree.map(lambda a: lax.all_gather(a, axis, axis=dim, tiled=True), shard)
    return absorb(state, everything, jnp.int32(0))


def local_trace(matrix_block, diagonal_mask):
    return jnp.sum(matrix_block * diagonal_mask)


def body(density_start, branches):
    rows_here, cols_here = density_start.shape
    row_first = lax.axis_index("row") * rows_here
    col_first = lax.axis_index("col") * cols_here
    row_ids = row_first + lax.broadcasted_iota(jnp.int32, (rows_here, cols_here), 0)
    col_ids = col_first + lax.broadcasted_iota(jnp.int32, (rows_here, cols_here), 1)
    diagonal_mask = (row_ids == col_ids).astype(jnp.float32)
    size_total = cols_here * lax.axis_size("col")
    density = density_start
    records = []
    for iteration in range(ITERS):
        narrow = density.astype(jnp.bfloat16)
        empty = jnp.zeros((rows_here, cols_here), jnp.float32)
        plain_local = local_trace(density, diagonal_mask)
        row_panel = lax.all_gather(narrow, "col", axis=1, tiled=True)

        def add_rows(accumulated, shard_piece, offset):
            panel_part = lax.dynamic_slice_in_dim(row_panel, offset, shard_piece.shape[0], 1)
            return accumulated + jnp.dot(
                panel_part, shard_piece, preferred_element_type=jnp.float32
            )

        square = taken_in(narrow, "row", 0, add_rows, empty)
        square_local = local_trace(square, diagonal_mask)
        branch_now = branches[iteration]
        records.append(jnp.stack([plain_local, square_local]))
        density = jnp.where(branch_now == 1, 2.0 * density - square, square)
    stacked = jnp.stack(records)
    stacked = lax.psum(stacked, ("row", "col"))
    occupations = stacked / size_total
    return (density, occupations)


def solution(mesh):
    in_specs = (P("row", "col"), P())
    out_specs = (P("row", "col"), P())
    return jax.shard_map(body, mesh=mesh, in_specs=in_specs, out_specs=out_specs, check_vma=False)
```

profile of v0, /device:TPU:0, one launch (start us, length us, event | category | flops | bytes accessed | tf_op | source)
XLA Modules:
  0.0 182.0 jit_solution(16147823306401190443)
XLA Ops:
  0.7 1.6 fusion.17
  6.1 13.7 %all_gather.36 = bf16[64,512]{1,0:T(8,128)(2,1)S(1)} all-gather(bf16[64,128]{1,0:T(8,128)(2,1)S(1)} %convert_element_type.19), channel_id=1, replica_groups=mesh['row'=8,'col'=4] {'col'}, dimensions={1}, use_global_device_ids=true | all-gather | bytes 81920 | tf_op jit(solution)/shard_map/all_gather | solution.py:32
  19.8 9.2 %all_gather.37 = bf16[512,128]{1,0:T(8,128)(2,1)S(1)} all-gather(bf16[64,128]{1,0:T(8,128)(2,1)S(1)} %convert_element_type.19), channel_id=1, replica_groups=mesh['row'=8,'col'=4] {'row'}, dimensions={0}, use_global_device_ids=true | all-gather | bytes 147456 | tf_op jit(solution)/shard_map/all_gather | solution.py:10
  29.0 0.2 fusion.16
  29.2 12.0 %all_gather.38 = bf16[64,512]{1,0:T(8,128)(2,1)S(1)} all-gather(bf16[64,128]{1,0:T(8,128)(2,1)S(1)} %get-tuple-element.24), channel_id=1, replica_groups=mesh['row'=8,'col'=4] {'col'}, dimensions={1}, use_global_device_ids=true | all-gather | bytes 81920 | tf_op jit(solution)/shard_map/all_gather | solution.py:32
  41.2 9.2 %all_gather.39 = bf16[512,128]{1,0:T(8,128)(2,1)S(1)} all-gather(bf16[64,128]{1,0:T(8,128)(2,1)S(1)} %get-tuple-element.24), channel_id=1, replica_groups=mesh['row'=8,'col'=4] {'row'}, dimensions={0}, use_global_device_ids=true | all-gather | bytes 147456 | tf_op jit(solution)/shard_map/all_gather | solution.py:10
  50.4 0.2 fusion.15
  50.5 12.0 %all_gather.40 = bf16[64,512]{1,0:T(8,128)(2,1)S(1)} all-gather(bf16[64,128]{1,0:T(8,128)(2,1)S(1)} %get-tuple-element.22), channel_id=1, replica_groups=mesh['row'=8,'col'=4] {'col'}, dimensions={1}, use_global_device_ids=true | all-gather | bytes 81920 | tf_op jit(solution)/shard_map/all_gather | solution.py:32
  62.5 8.2 %all_gather.41 = bf16[512,128]{1,0:T(8,128)(2,1)S(1)} all-gather(bf16[64,128]{1,0:T(8,128)(2,1)S(1)} %get-tuple-element.22), channel_id=1, replica_groups=mesh['row'=8,'col'=4] {'row'}, dimensions={0}, use_global_device_ids=true | all-gather | bytes 147456 | tf_op jit(solution)/shard_map/all_gather | solution.py:10
  70.7 0.2 fusion.14
  70.9 12.0 %all_gather.42 = bf16[64,512]{1,0:T(8,128)(2,1)S(1)} all-gather(bf16[64,128]{1,0:T(8,128)(2,1)S(1)} %get-tuple-element.20), channel_id=1, replica_groups=mesh['row'=8,'col'=4] {'col'}, dimensions={1}, use_global_device_ids=true | all-gather | bytes 81920 | tf_op jit(solution)/shard_map/all_gather | solution.py:32
  82.9 9.2 %all_gather.43 = bf16[512,128]{1,0:T(8,128)(2,1)S(1)} all-gather(bf16[64,128]{1,0:T(8,128)(2,1)S(1)} %get-tuple-element.20), channel_id=1, replica_groups=mesh['row'=8,'col'=4] {'row'}, dimensions={0}, use_global_device_ids=true | all-gather | bytes 147456 | tf_op jit(solution)/shard_map/all_gather | solution.py:10
  92.1 0.2 fusion.13
  92.2 12.0 %all_gather.44 = bf16[64,512]{1,0:T(8,128)(2,1)S(1)} all-gather(bf16[64,128]{1,0:T(8,128)(2,1)S(1)} %get-tuple-element.18), channel_id=1, replica_groups=mesh['row'=8,'col'=4] {'col'}, dimensions={1}, use_global_device_ids=true | all-gather | bytes 81920 | tf_op jit(solution)/shard_map/all_gather | solution.py:32
  104.2 8.2 %all_gather.45 = bf16[512,128]{1,0:T(8,128)(2,1)S(1)} all-gather(bf16[64,128]{1,0:T(8,128)(2,1)S(1)} %get-tuple-element.18), channel_id=1, replica_groups=mesh['row'=8,'col'=4] {'row'}, dimensions={0}, use_global_device_ids=true | all-gather | bytes 147456 | tf_op jit(solution)/shard_map/all_gather | solution.py:10
  112.4 0.2 fusion.12
  112.6 12.0 %all_gather.46 = bf16[64,512]{1,0:T(8,128)(2,1)S(1)} all-gather(bf16[64,128]{1,0:T(8,128)(2,1)S(1)} %get-tuple-element.16), channel_id=1, replica_groups=mesh['row'=8,'col'=4] {'col'}, dimensions={1}, use_global_device_ids=true | all-gather | bytes 81920 | tf_op jit(solution)/shard_map/all_gather | solution.py:32
  124.6 9.2 %all_gather.47 = bf16[512,128]{1,0:T(8,128)(2,1)S(1)} all-gather(bf16[64,128]{1,0:T(8,128)(2,1)S(1)} %get-tuple-element.16), channel_id=1, replica_groups=mesh['row'=8,'col'=4] {'row'}, dimensions={0}, use_global_device_ids=true | all-gather | bytes 147456 | tf_op jit(solution)/shard_map/all_gather | solution.py:10
  133.8 1.5 fusion.10
  135.2 1.3 maximum_bitcast_fusion.5
  136.5 0.1 copy.10
  136.6 1.3 maximum_bitcast_fusion.4
  138.1 1.3 maximum_bitcast_fusion.3
  139.4 0.1 copy.8
  139.4 1.3 maximum_bitcast_fusion.2
  140.8 0.1 copy.7
  140.9 1.3 maximum_bitcast_fusion.1
  142.3 1.3 maximum_bitcast_fusion
  143.6 0.1 copy.5
  143.7 0.1 stack.99
  143.8 37.7 %psum.7 = f32[6,2]{0,1:T(2,128)S(1)} all-reduce(f32[6,2]{0,1:T(2,128)S(1)} %stack.99), channel_id=1, replica_groups=mesh['row'=8,'col'=4] {'row','col'}, use_global_device_ids=true, to_apply=%region_12.13 | all-reduce | flops 12 | bytes 96 | tf_op jit(solution)/shard_map/psum | solution.py:46
  181.5 0.6 broadcast_multiply_fusion
  (7 shorter events, 0.2 us)
Async XLA Ops:
  0.6 5.5 %copy-start = (f32[64,128]{1,0:T(8,128)S(1)}, f32[64,128]{1,0:T(8,128)}, u32[]{:S(2)}) copy-start(f32[64,128]{1,0:T(8,128)} %param.2) | copy-start | bytes 98308
where the time goes:
time: 183 us; the launch traced here: 182 us
  blocking collectives  165 us (90%)
  other arithmetic  8.46 us (5%)
  between operations  4.56 us (2%)
  matrix products  2.26 us (1%)
  local copies, waits for them, and re-layouts  2.23 us (1%)
    all_gather x6, blocking collectives, body(): row_panel = lax.all_gather(narrow, 'col', axis=1, tiled=True)  73.7 us
    all_gather x6, blocking collectives, taken_in(): lax.all_gather(a, axis, axis=dim, tiled=True)  53.2 us
    psum x1, blocking collectives, body(): stacked = lax.psum(stacked, ('row', 'col'))  37.7 us
    another operation x6, other arithmetic, body(): stacked = jnp.stack(records)  7.88 us

commit v1 on v0

--- a/solution.py
+++ b/solution.py
@@ -43,7 +43,7 @@
         records.append(jnp.stack([plain_local, square_local]))
         density = jnp.where(branch_now == 1, 2.0 * density - square, square)
     stacked = jnp.stack(records)
-    stacked = lax.psum(stacked, ("row", "col"))
+    stacked = lax.all_gather(stacked, ("row", "col")).sum(axis=0)
     occupations = stacked / size_total
     return (density, occupations)
 

time: 183 us -> 209 us (1.14)
  blocking collectives: 165 us -> 191 us
    all_gather x0 -> x1, blocking collectives: none -> 64.2 us  [body(): stacked = lax.all_gather(stacked, ('row', 'col')).sum(axis=0)]
    psum x1 -> x0, blocking collectives: 37.7 us -> none  [body(): stacked = lax.psum(stacked, ('row', 'col'))]
where the time goes in v1:
time: 209 us
  blocking collectives  191 us (91%)
  other arithmetic  8.5 us (4%)
  between operations  4.56 us (2%)
  matrix products  2.26 us (1%)
  local copies, waits for them, and re-layouts  2.23 us (1%)
    all_gather x6, blocking collectives, body(): row_panel = lax.all_gather(narrow, 'col', axis=1, tiled=True)  73.7 us
    all_gather x1, blocking collectives, body(): stacked = lax.all_gather(stacked, ('row', 'col')).sum(axis=0)  64.2 us
    all_gather x6, blocking collectives, taken_in(): lax.all_gather(a, axis, axis=dim, tiled=True)  53.2 us
    another operation x6, other arithmetic, body(): stacked = jnp.stack(records)  7.88 us

profile of v1, /device:TPU:0, one launch (start us, length us, event | category | flops | bytes accessed | tf_op | source)
XLA Modules:
  0.0 208.6 jit_solution(3072413517566236486)
XLA Ops:
  0.7 1.6 fusion.17
  6.1 13.7 %all_gather.42 = bf16[64,512]{1,0:T(8,128)(2,1)S(1)} all-gather(bf16[64,128]{1,0:T(8,128)(2,1)S(1)} %convert_element_type.19), channel_id=1, replica_groups=mesh['row'=8,'col'=4] {'col'}, dimensions={1}, use_global_device_ids=true | all-gather | bytes 81920 | tf_op jit(solution)/shard_map/all_gather | solution.py:32
  19.8 9.2 %all_gather.43 = bf16[512,128]{1,0:T(8,128)(2,1)S(1)} all-gather(bf16[64,128]{1,0:T(8,128)(2,1)S(1)} %convert_element_type.19), channel_id=1, replica_groups=mesh['row'=8,'col'=4] {'row'}, dimensions={0}, use_global_device_ids=true | all-gather | bytes 147456 | tf_op jit(solution)/shard_map/all_gather | solution.py:10
  29.0 0.2 fusion.16
  29.2 12.0 %all_gather.44 = bf16[64,512]{1,0:T(8,128)(2,1)S(1)} all-gather(bf16[64,128]{1,0:T(8,128)(2,1)S(1)} %get-tuple-element.22), channel_id=1, replica_groups=mesh['row'=8,'col'=4] {'col'}, dimensions={1}, use_global_device_ids=true | all-gather | bytes 81920 | tf_op jit(solution)/shard_map/all_gather | solution.py:32
  41.2 9.2 %all_gather.45 = bf16[512,128]{1,0:T(8,128)(2,1)S(1)} all-gather(bf16[64,128]{1,0:T(8,128)(2,1)S(1)} %get-tuple-element.22), channel_id=1, replica_groups=mesh['row'=8,'col'=4] {'row'}, dimensions={0}, use_global_device_ids=true | all-gather | bytes 147456 | tf_op jit(solution)/shard_map/all_gather | solution.py:10
  50.4 0.2 fusion.15
  50.5 12.0 %all_gather.46 = bf16[64,512]{1,0:T(8,128)(2,1)S(1)} all-gather(bf16[64,128]{1,0:T(8,128)(2,1)S(1)} %get-tuple-element.20), channel_id=1, replica_groups=mesh['row'=8,'col'=4] {'col'}, dimensions={1}, use_global_device_ids=true | all-gather | bytes 81920 | tf_op jit(solution)/shard_map/all_gather | solution.py:32
  62.5 8.2 %all_gather.47 = bf16[512,128]{1,0:T(8,128)(2,1)S(1)} all-gather(bf16[64,128]{1,0:T(8,128)(2,1)S(1)} %get-tuple-element.20), channel_id=1, replica_groups=mesh['row'=8,'col'=4] {'row'}, dimensions={0}, use_global_device_ids=true | all-gather | bytes 147456 | tf_op jit(solution)/shard_map/all_gather | solution.py:10
  70.7 0.2 fusion.14
  70.9 12.0 %all_gather.48 = bf16[64,512]{1,0:T(8,128)(2,1)S(1)} all-gather(bf16[64,128]{1,0:T(8,128)(2,1)S(1)} %get-tuple-element.18), channel_id=1, replica_groups=mesh['row'=8,'col'=4] {'col'}, dimensions={1}, use_global_device_ids=true | all-gather | bytes 81920 | tf_op jit(solution)/shard_map/all_gather | solution.py:32
  82.9 9.2 %all_gather.49 = bf16[512,128]{1,0:T(8,128)(2,1)S(1)} all-gather(bf16[64,128]{1,0:T(8,128)(2,1)S(1)} %get-tuple-element.18), channel_id=1, replica_groups=mesh['row'=8,'col'=4] {'row'}, dimensions={0}, use_global_device_ids=true | all-gather | bytes 147456 | tf_op jit(solution)/shard_map/all_gather | solution.py:10
  92.1 0.2 fusion.13
  92.2 12.0 %all_gather.50 = bf16[64,512]{1,0:T(8,128)(2,1)S(1)} all-gather(bf16[64,128]{1,0:T(8,128)(2,1)S(1)} %get-tuple-element.16), channel_id=1, replica_groups=mesh['row'=8,'col'=4] {'col'}, dimensions={1}, use_global_device_ids=true | all-gather | bytes 81920 | tf_op jit(solution)/shard_map/all_gather | solution.py:32
  104.2 8.2 %all_gather.51 = bf16[512,128]{1,0:T(8,128)(2,1)S(1)} all-gather(bf16[64,128]{1,0:T(8,128)(2,1)S(1)} %get-tuple-element.16), channel_id=1, replica_groups=mesh['row'=8,'col'=4] {'row'}, dimensions={0}, use_global_device_ids=true | all-gather | bytes 147456 | tf_op jit(solution)/shard_map/all_gather | solution.py:10
  112.4 0.2 fusion.12
  112.6 12.0 %all_gather.52 = bf16[64,512]{1,0:T(8,128)(2,1)S(1)} all-gather(bf16[64,128]{1,0:T(8,128)(2,1)S(1)} %get-tuple-element.14), channel_id=1, replica_groups=mesh['row'=8,'col'=4] {'col'}, dimensions={1}, use_global_device_ids=true | all-gather | bytes 81920 | tf_op jit(solution)/shard_map/all_gather | solution.py:32
  124.6 9.2 %all_gather.53 = bf16[512,128]{1,0:T(8,128)(2,1)S(1)} all-gather(bf16[64,128]{1,0:T(8,128)(2,1)S(1)} %get-tuple-element.14), channel_id=1, replica_groups=mesh['row'=8,'col'=4] {'row'}, dimensions={0}, use_global_device_ids=true | all-gather | bytes 147456 | tf_op jit(solution)/shard_map/all_gather | solution.py:10
  133.8 1.5 fusion.10
  135.2 1.3 maximum_bitcast_fusion.5
  136.5 0.1 copy.10
  136.6 1.3 maximum_bitcast_fusion.4
  138.1 1.3 maximum_bitcast_fusion.3
  139.4 0.1 copy.8
  139.4 1.3 maximum_bitcast_fusion.2
  140.8 0.1 copy.7
  140.9 1.3 maximum_bitcast_fusion.1
  142.3 1.3 maximum_bitcast_fusion
  143.6 0.1 copy.5
  143.7 0.1 stack.99
  143.8 64.2 %all-gather.1 = f32[32,6,2]{1,2,0:T(2,128)S(1)} all-gather(f32[1,6,2]{1,2,0:T(2,128)S(1)} %bitcast.43), channel_id=2, replica_groups=mesh['row'=8,'col'=4] {'row','col'}, dimensions={0}, use_global_device_ids=true | all-gather | bytes 1584 | tf_op jit(solution)/shard_map/all_gather | solution.py:46
  208.0 0.6 broadcast_multiply_fusion
  (8 shorter events, 0.3 us)
Async XLA Ops:
  0.6 5.5 %copy-start = (f32[64,128]{1,0:T(8,128)S(1)}, f32[64,128]{1,0:T(8,128)}, u32[]{:S(2)}) copy-start(f32[64,128]{1,0:T(8,128)} %param.2) | copy-start | bytes 98308
